TPU v7x, 32 devices: a whole 2x2x4 slice. The times are simulated.
32 devices in a mesh: seq: 2 (over x), row: 4 (over y, core), col: 4 (over z).
Axes of the slice: x: 2, y: 2, z: 4, core: 2. Of those that a mesh axis runs over, the one named last changes fastest.
Arguments:
- activations: bfloat16 [2, 64, 8192], P(None, 'row', 'seq'), may hold values from -6 to 6
- gradients: bfloat16 [2, 64, 8192], P(None, 'col', 'seq'), may hold values from -6 to 6
- basis_in: bfloat16 [8192, 4096], P('seq', 'col'), may hold values from -0.0625 to 0.0625
- basis_out: bfloat16 [8192, 4096], P('seq', 'row'), may hold values from -0.0625 to 0.0625
- lengths: int32 [2], replicated, may hold values from 16 to 64
Outputs:
- corrections: float32 [4096, 4096], P(('row', 'seq'), 'col')
All inputs are finite; a program needn't handle non-finite values.
Results may differ from a plain program's by a relative error of at most 0.0023.
Values may be sent and summed in bfloat16 or wider, within the bound.
No kernel may reach another device: no remote copies, remote signals or barrier semaphores. Data moves between devices by JAX's collectives and lax.ppermute only.
A program may use at most 64 MiB of HBM per device.

v0:
```python
import jax
import jax.numpy as jnp
from jax import lax
from jax.sharding import PartitionSpec as P


def turned_terms(tokens, basis):
    return jnp.einsum("ntf,fk->ntk", tokens, basis, preferred_element_type=jnp.float32)


def local(activations, gradients, basis_in, basis_out, lengths):
    seq_count = lax.axis_size("seq")
    seq_index = lax.axis_index("seq")
    length = lengths[seq_index]
    summed_in = lax.psum_scatter(
        turned_terms(activations, basis_in), "seq", scatter_dimension=0, tiled=True
    )
    turned_in = summed_in[0].astype(jnp.bfloat16)
    summed_out = lax.psum_scatter(
        turned_terms(gradients, basis_out), "seq", scatter_dimension=0, tiled=True
    )
    turned_out = summed_out[0].astype(jnp.bfloat16)
    every_in = lax.all_gather(turned_in, "row", axis=0, tiled=True)
    every_out = lax.all_gather(turned_out, "col", axis=0, tiled=True)
    slot_total = every_in.shape[0]
    slots = jnp.arange(slot_total)
    contract = (((0,), (0,)), ((), ()))
    kept = jnp.where((slots < length)[:, None], every_out, jnp.zeros((), jnp.bfloat16))
    product_tile = lax.dot_general(kept, every_in, contract, preferred_element_type=jnp.float32)
    squared = product_tile * product_tile / (seq_count * slot_total)
    return lax.psum_scatter(squared, "seq", scatter_dimension=0, tiled=True)


def solution(mesh):
    return jax.shard_map(
        local,
        mesh=mesh,
        in_specs=(
            P(None, "row", "seq"),
            P(None, "col", "seq"),
            P("seq", "col"),
            P("seq", "row"),
            P(),
        ),
        out_specs=P(("row", "seq"), "col"),
        check_vma=False,
    )
```

profile of v0, /device:TPU:0, one launch (start us, length us, event | category | flops | bytes accessed | tf_op | source)
XLA Modules:
  0.0 117.2 jit_solution(11242291318039714321)
XLA Ops:
  6.5 0.0 copy-start
  6.5 0.0 copy-start.1
  6.5 0.0 reduce-scatter.6.cloned.1.call-start
  6.5 0.9 copy-done
  7.5 5.6 %fusion = f32[2,16,1024]{2,1,0:T(8,128)} fusion(bf16[2,16,4096]{2,1,0:T(8,128)(2,1)S(1)} %copy-done, bf16[4096,1024]{1,0:T(8,128)(2,1)} %param.7), kind=kOutput, calls=%fused_computation | convolution fusion | flops 268435456 | bytes 8781824 | tf_op jit(solution)/shard_map/ntf,fk->ntk/dot_general | solution.py:8
  13.1 0.0 copy-start.2
  13.1 0.0 reduce-scatter.6.cloned.1.call-update
  13.1 0.0 reduce-scatter.4.cloned.1.call-start
  13.1 0.0 copy-done.1
  13.2 5.6 %fusion.2 = f32[2,16,1024]{2,1,0:T(8,128)} fusion(bf16[2,16,4096]{2,1,0:T(8,128)(2,1)S(1)} %copy-done.1, bf16[4096,1024]{1,0:T(8,128)(2,1)} %param.8), kind=kOutput, calls=%fused_computation.2 | convolution fusion | flops 268435456 | bytes 8781824 | tf_op jit(solution)/shard_map/ntf,fk->ntk/dot_general | solution.py:8
  18.7 0.0 reduce-scatter.4.cloned.1.call-update
  18.8 0.0 reduce-scatter.8.cloned.1.call-start
  18.8 0.0 copy-done.2
  18.8 0.7 dynamic_slice.3
  19.5 0.7 iota_compare_fusion
  20.2 6.1 %reduce-scatter.6.cloned.1.call-done = f32[1,16,1024]{2,1,0:T(8,128)} async-done(((f32[2,16,1024]{2,1,0:T(8,128)}), f32[1,16,1024]{2,1,0:T(8,128)}) %reduce-scatter.6.cloned.1.call-update) | async-done | bytes 65552 | tf_op jit(solution)/shard_map/reduce_scatter | solution.py:15
  26.3 0.8 convert_element_type.14
  27.2 5.4 %all-gather.1 = bf16[1,64,1024]{2,1,0:T(8,128)(2,1)S(1)} all-gather(bf16[1,16,1024]{2,1,0:T(8,128)(2,1)S(1)} %convert_element_type.14), channel_id=3, replica_groups=mesh['seq'=2,'row'=4,'col'=4] {'row'}, dimensions={1}, use_global_device_ids=true | all-gather | bytes 163840 | tf_op jit(solution)/shard_map/all_gather | solution.py:23
  32.6 6.4 %reduce-scatter.4.cloned.1.call-done = f32[1,16,1024]{2,1,0:T(8,128)} async-done(((f32[2,16,1024]{2,1,0:T(8,128)}), f32[1,16,1024]{2,1,0:T(8,128)}) %reduce-scatter.4.cloned.1.call-update) | async-done | bytes 65552 | tf_op jit(solution)/shard_map/reduce_scatter | solution.py:19
  38.9 0.8 convert_element_type.12
  39.8 13.4 %all-gather = bf16[1,64,1024]{2,1,0:T(8,128)(2,1)S(1)} all-gather(bf16[1,16,1024]{2,1,0:T(8,128)(2,1)S(1)} %convert_element_type.12), channel_id=2, replica_groups=mesh['seq'=2,'row'=4,'col'=4] {'col'}, dimensions={1}, use_global_device_ids=true | all-gather | bytes 163840 | tf_op jit(solution)/shard_map/all_gather | solution.py:24
  53.2 2.8 %multiply_multiply_fusion = f32[1024,1024]{1,0:T(8,128)} fusion(bf16[1,64,1024]{2,1,0:T(8,128)(2,1)S(1)} %all-gather.1, bf16[1,64,1024]{2,1,0:T(8,128)(2,1)S(1)} %all-gather, pred[64]{0:T(512)(128)(4,1)S(1)} %iota_compare_fusion), kind=kOutput, calls=%fused_computation.4 | convolution fusion | flops 136380416 | bytes 4456512 | tf_op jit(solution)/shard_map/dot_general | solution.py:29
  56.0 0.0 reduce-scatter.8.cloned.1.call-update
  56.0 54.7 %reduce-scatter.8.cloned.1.call-done = f32[512,1024]{1,0:T(8,128)} async-done(((f32[1024,1024]{1,0:T(8,128)}), f32[512,1024]{1,0:T(8,128)}) %reduce-scatter.8.cloned.1.call-update) | async-done | bytes 2097168 | tf_op jit(solution)/shard_map/reduce_scatter | solution.py:31
Async XLA Ops:
  6.5 1.0 copy-start
  6.5 6.6 %copy-start.1 = (bf16[2,16,4096]{2,1,0:T(8,128)(2,1)S(1)}, bf16[2,16,4096]{2,1,0:T(8,128)(2,1)}, u32[]{:S(2)}) copy-start(bf16[2,16,4096]{2,1,0:T(8,128)(2,1)} %param.6) | copy-start | bytes 786436
  6.5 19.8 %reduce-scatter.6.cloned.1.call-start = ((), (), s32[]{:S(2)}) async-start(), calls=%async_computation.4 | async-start | bytes 196608 | tf_op jit(solution)/shard_map/reduce_scatter | solution.py:15
  13.1 5.7 %copy-start.2 = (s32[2]{0:T(128)S(1)}, s32[2]{0:T(128)}, u32[]{:S(2)}) copy-start(s32[2]{0:T(128)} %param.9) | copy-start | bytes 28
  13.1 25.8 %reduce-scatter.4.cloned.1.call-start = ((), (), s32[]{:S(2)}) async-start(), calls=%async_computation.3 | async-start | bytes 196608 | tf_op jit(solution)/shard_map/reduce_scatter | solution.py:19
  18.8 92.0 %reduce-scatter.8.cloned.1.call-start = ((), (), s32[]{:S(2)}) async-start(), calls=%async_computation.5 | async-start | bytes 6291456 | tf_op jit(solution)/shard_map/reduce_scatter | solution.py:31
Sparse Core Ops, SparseCore 0:
  13.2 13.0 reduce-scatter.5
  28.5 10.3 reduce-scatter.3
  56.1 54.5 reduce-scatter.7
where the time goes:
time: 118 us; the launch traced here: 117 us
  waiting for transfers between devices  67.3 us (57%)
  blocking collectives  18.8 us (16%)
  matrix products  13.9 us (12%)
  between operations  13.1 us (11%)
  other arithmetic  2.38 us (2%)
  local copies, waits for them, and re-layouts  1.62 us (1%)
    reduce_scatter x1, waiting for transfers between devices, local(): return lax.psum_scatter(squared, 'seq', scatter_dimension=0, tiled=True)  54.7 us
    all_gather x1, blocking collectives, local(): every_out = lax.all_gather(turned_out, 'col', axis=0, tiled=True)  13.4 us
    dot_general x2, matrix products, turned_terms(): jnp.einsum('ntf,fk->ntk', tokens, basis, preferred_element_type=jnp.float32)  11.2 us
    reduce_scatter x1, waiting for transfers between devices, local(): lax.psum_scatter(turned_terms(gradients, basis_out), 'seq', scatter_dimen...  6.36 us
    reduce_scatter x1, waiting for transfers between devices, local(): lax.psum_scatter(turned_terms(activations, basis_in), 'seq', scatter_dime...  6.15 us
    all_gather x1, blocking collectives, local(): every_in = lax.all_gather(turned_in, 'row', axis=0, tiled=True)  5.4 us
    dot_general x1, matrix products, local(): lax.dot_general(kept, every_in, contract, preferred_element_type=jnp.floa...  2.75 us
  transfers between devices with their start and end apart: 3, of which 3 were waited for; matrix products, arithmetic and copies ran while one was open for 7% of the time, Pallas kernels for 0%

commit v1 on v0

--- a/solution.py
+++ b/solution.py
@@ -21,7 +21,12 @@
     )
     turned_out = summed_out[0].astype(jnp.bfloat16)
     every_in = lax.all_gather(turned_in, "row", axis=0, tiled=True)
-    every_out = lax.all_gather(turned_out, "col", axis=0, tiled=True)
+    ring = [turned_out]
+    for hop in range(3):
+        ring.append(lax.ppermute(ring[-1], "col", [(dev, (dev + 1) % 4) for dev in range(4)]))
+    every_out = jnp.roll(
+        jnp.concatenate(ring[::-1], axis=0), (lax.axis_index("col") + 1) * ring[0].shape[0], axis=0
+    )
     slot_total = every_in.shape[0]
     slots = jnp.arange(slot_total)
     contract = (((0,), (0,)), ((), ()))

time: 118 us -> 112 us (0.949)
  blocking collectives: 18.8 us -> 5.4 us
  starting transfers between devices: 0.09 us -> 3.05 us
  waiting for transfers between devices: 67.3 us -> 70.1 us
  other arithmetic: 2.38 us -> 4.07 us
    all_gather x1 -> x0, blocking collectives: 13.4 us -> none  [local(): every_out = lax.all_gather(turned_out, 'col', axis=0, tiled=True)]
    ppermute x0 -> x3, waiting for transfers between devices: none -> 3.57 us  [local(): lax.ppermute(ring[-1], 'col', [(dev, (dev + 1) % 4) for dev in range(4)])]
    ppermute x0 -> x3, starting transfers between devices: none -> 2.97 us  [local(): lax.ppermute(ring[-1], 'col', [(dev, (dev + 1) % 4) for dev in range(4)])]
  transfers between devices with their start and end apart: 3 -> 6, of which waited for: 3 -> 4; matrix products, arithmetic and copies ran while one was open for 7% -> 8% of each run, Pallas kernels for 0% -> 0%
where the time goes in v1:
time: 112 us; the launch traced here: 111 us
  waiting for transfers between devices  70.1 us (63%)
  matrix products  13.9 us (12%)
  between operations  13.2 us (12%)
  blocking collectives  5.4 us (5%)
  other arithmetic  4.07 us (4%)
  starting transfers between devices  3.05 us (3%)
  local copies, waits for them, and re-layouts  1.64 us (1%)
    reduce_scatter x1, waiting for transfers between devices, local(): return lax.psum_scatter(squared, 'seq', scatter_dimension=0, tiled=True)  53.6 us
    dot_general x2, matrix products, turned_terms(): jnp.einsum('ntf,fk->ntk', tokens, basis, preferred_element_type=jnp.float32)  11.2 us
    reduce_scatter x1, waiting for transfers between devices, local(): lax.psum_scatter(turned_terms(gradients, basis_out), 'seq', scatter_dimen...  7.52 us
    all_gather x1, blocking collectives, local(): every_in = lax.all_gather(turned_in, 'row', axis=0, tiled=True)  5.4 us
    reduce_scatter x1, waiting for transfers between devices, local(): lax.psum_scatter(turned_terms(activations, basis_in), 'seq', scatter_dime...  5.32 us
    ppermute x3, waiting for transfers between devices, local(): lax.ppermute(ring[-1], 'col', [(dev, (dev + 1) % 4) for dev in range(4)])  3.57 us
    ppermute x3, starting transfers between devices, local(): lax.ppermute(ring[-1], 'col', [(dev, (dev + 1) % 4) for dev in range(4)])  2.97 us
    dot_general x1, matrix products, local(): lax.dot_general(kept, every_in, contract, preferred_element_type=jnp.floa...  2.75 us
  transfers between devices with their start and end apart: 6, of which 4 were waited for; matrix products, arithmetic and copies ran while one was open for 8% of the time, Pallas kernels for 0%

profile of v1, /device:TPU:0, one launch (start us, length us, event | category | flops | bytes accessed | tf_op | source)
XLA Modules:
  0.0 111.3 jit_solution(13100850115560379669)
XLA Ops:
  6.5 0.0 copy-start
  6.5 0.0 copy-start.1
  6.5 0.0 reduce-scatter.4.cloned.1.call-start
  6.5 0.9 copy-done
  7.5 5.6 %fusion.2 = f32[2,16,1024]{2,1,0:T(8,128)} fusion(bf16[2,16,4096]{2,1,0:T(8,128)(2,1)S(1)} %copy-done, bf16[4096,1024]{1,0:T(8,128)(2,1)} %param.8), kind=kOutput, calls=%fused_computation.2 | convolution fusion | flops 268435456 | bytes 8781824 | tf_op jit(solution)/shard_map/ntf,fk->ntk/dot_general | solution.py:8
  13.1 0.0 copy-start.2
  13.1 0.0 reduce-scatter.4.cloned.1.call-update
  13.1 0.0 reduce-scatter.6.cloned.1.call-start
  13.1 0.0 copy-done.1
  13.1 5.6 %fusion = f32[2,16,1024]{2,1,0:T(8,128)} fusion(bf16[2,16,4096]{2,1,0:T(8,128)(2,1)S(1)} %copy-done.1, bf16[4096,1024]{1,0:T(8,128)(2,1)} %param.7), kind=kOutput, calls=%fused_computation | convolution fusion | flops 268435456 | bytes 8781824 | tf_op jit(solution)/shard_map/ntf,fk->ntk/dot_general | solution.py:8
  18.7 0.0 reduce-scatter.6.cloned.1.call-update
  18.8 0.0 reduce-scatter.8.cloned.1.call-start
  18.8 7.5 %reduce-scatter.4.cloned.1.call-done = f32[1,16,1024]{2,1,0:T(8,128)} async-done(((f32[2,16,1024]{2,1,0:T(8,128)}), f32[1,16,1024]{2,1,0:T(8,128)}) %reduce-scatter.4.cloned.1.call-update) | async-done | bytes 65552 | tf_op jit(solution)/shard_map/reduce_scatter | solution.py:19
  26.3 0.8 convert_bitcast_fusion
  27.2 1.5 %collective-permute-start = (bf16[16,1024]{1,0:T(8,128)(2,1)S(1)}, bf16[16,1024]{1,0:T(8,128)(2,1)S(1)}, u32[]{:S(2)}, u32[]{:S(2)}) collective-permute-start(bf16[16,1024]{1,0:T(8,128)(2,1)S(1)} %convert_bitcast_fusion), channel_id=1, source_target_pairs={{0,1},{1,2},{2,3},{3,0},{4,5},{5,6},{6,7},{7,4},{8,9},{9,10},{10,1... | collective-permute-start | bytes 98312 | tf_op jit(solution)/shard_map/ppermute | solution.py:26
  28.7 0.0 copy-done.2
  28.7 0.7 dynamic_slice.7
  29.3 3.6 %collective-permute-done = bf16[16,1024]{1,0:T(8,128)(2,1)S(1)} collective-permute-done((bf16[16,1024]{1,0:T(8,128)(2,1)S(1)}, bf16[16,1024]{1,0:T(8,128)(2,1)S(1)}, u32[]{:S(2)}, u32[]{:S(2)}) %collective-permute-start) | collective-permute-done | bytes 32800 | tf_op jit(solution)/shard_map/ppermute | solution.py:26
  32.9 0.0 collective-permute-start.1
  32.9 0.7 iota_compare_fusion
  33.6 5.3 %reduce-scatter.6.cloned.1.call-done = f32[1,16,1024]{2,1,0:T(8,128)} async-done(((f32[2,16,1024]{2,1,0:T(8,128)}), f32[1,16,1024]{2,1,0:T(8,128)}) %reduce-scatter.6.cloned.1.call-update) | async-done | bytes 65552 | tf_op jit(solution)/shard_map/reduce_scatter | solution.py:15
  38.9 0.8 convert_element_type.14
  39.8 0.0 collective-permute-done.1
  39.8 1.5 %collective-permute-start.2 = (bf16[16,1024]{1,0:T(8,128)(2,1)S(1)}, bf16[16,1024]{1,0:T(8,128)(2,1)S(1)}, u32[]{:S(2)}, u32[]{:S(2)}) collective-permute-start(bf16[16,1024]{1,0:T(8,128)(2,1)S(1)} %collective-permute-done.1), channel_id=1, source_target_pairs={{0,1},{1,2},{2,3},{3,0},{4,5},{5,6},{6,7},{7,4},{8,9},{9,10},{10,1... | collective-permute-start | bytes 98312 | tf_op jit(solution)/shard_map/ppermute | solution.py:26
  41.3 5.4 %all-gather = bf16[1,64,1024]{2,1,0:T(8,128)(2,1)S(1)} all-gather(bf16[1,16,1024]{2,1,0:T(8,128)(2,1)S(1)} %convert_element_type.14), channel_id=2, replica_groups=mesh['seq'=2,'row'=4,'col'=4] {'row'}, dimensions={1}, use_global_device_ids=true | all-gather | bytes 163840 | tf_op jit(solution)/shard_map/all_gather | solution.py:23
  46.7 0.0 collective-permute-done.2
  46.7 0.8 constant_dynamic-update-slice_fusion.4
  47.6 0.8 constant_dynamic-update-slice_fusion
  48.4 2.7 %multiply_multiply_fusion = f32[1024,1024]{1,0:T(8,128)} fusion(bf16[1,64,1024]{2,1,0:T(8,128)(2,1)S(1)} %all-gather, bf16[128,1024]{1,0:T(8,128)(2,1)S(1)} %constant_dynamic-update-slice_fusion, s32[]{:T(128)S(6)} %select_n.22, pred[64]{0:T(512)(128)(4,1)S(1)} %iota_compare_fusion), kind=kOutput, calls=%fused_computation.4 | convolution fusion | flops 136380416 | bytes 4456964 | tf_op jit(solution)/shard_map/dot_general | solution.py:34
  51.1 0.0 reduce-scatter.8.cloned.1.call-update
  51.2 53.6 %reduce-scatter.8.cloned.1.call-done = f32[512,1024]{1,0:T(8,128)} async-done(((f32[1024,1024]{1,0:T(8,128)}), f32[512,1024]{1,0:T(8,128)}) %reduce-scatter.8.cloned.1.call-update) | async-done | bytes 2097168 | tf_op jit(solution)/shard_map/reduce_scatter | solution.py:36
  (6 shorter events, 0.0 us)
Async XLA Ops:
  6.5 1.0 copy-start
  6.5 6.6 %copy-start.1 = (bf16[2,16,4096]{2,1,0:T(8,128)(2,1)S(1)}, bf16[2,16,4096]{2,1,0:T(8,128)(2,1)}, u32[]{:S(2)}) copy-start(bf16[2,16,4096]{2,1,0:T(8,128)(2,1)} %param.5) | copy-start | bytes 786436
  6.5 19.8 %reduce-scatter.4.cloned.1.call-start = ((), (), s32[]{:S(2)}) async-start(), calls=%async_computation.3 | async-start | bytes 196608 | tf_op jit(solution)/shard_map/reduce_scatter | solution.py:19
  13.1 15.6 %copy-start.2 = (s32[2]{0:T(128)S(1)}, s32[2]{0:T(128)}, u32[]{:S(2)}) copy-start(s32[2]{0:T(128)} %param.9) | copy-start | bytes 28
  13.1 25.8 %reduce-scatter.6.cloned.1.call-start = ((), (), s32[]{:S(2)}) async-start(), calls=%async_computation.4 | async-start | bytes 196608 | tf_op jit(solution)/shard_map/reduce_scatter | solution.py:15
  18.8 86.0 %reduce-scatter.8.cloned.1.call-start = ((), (), s32[]{:S(2)}) async-start(), calls=%async_computation.5 | async-start | bytes 6291456 | tf_op jit(solution)/shard_map/reduce_scatter | solution.py:36
  27.2 5.7 %collective-permute-start = (bf16[16,1024]{1,0:T(8,128)(2,1)S(1)}, bf16[16,1024]{1,0:T(8,128)(2,1)S(1)}, u32[]{:S(2)}, u32[]{:S(2)}) collective-permute-start(bf16[16,1024]{1,0:T(8,128)(2,1)S(1)} %convert_bitcast_fusion), channel_id=1, source_target_pairs={{0,1},{1,2},{2,3},{3,0},{4,5},{5,6},{6,7},{7,4},{8,9},{9,10},{10,1... | collective-permute-start | bytes 98312 | tf_op jit(solution)/shard_map/ppermute | solution.py:26
  32.9 6.9 %collective-permute-start.1 = (bf16[16,1024]{1,0:T(8,128)(2,1)S(1)}, bf16[16,1024]{1,0:T(8,128)(2,1)S(1)}, u32[]{:S(2)}, u32[]{:S(2)}) collective-permute-start(bf16[16,1024]{1,0:T(8,128)(2,1)S(1)} %collective-permute-done), channel_id=1, source_target_pairs={{0,1},{1,2},{2,3},{3,0},{4,5},{5,6},{6,7},{7,4},{8,9},{9,10},{10,1... | collective-permute-start | bytes 98312 | tf_op jit(solution)/shard_map/ppermute | solution.py:26
  39.8 6.9 %collective-permute-start.2 = (bf16[16,1024]{1,0:T(8,128)(2,1)S(1)}, bf16[16,1024]{1,0:T(8,128)(2,1)S(1)}, u32[]{:S(2)}, u32[]{:S(2)}) collective-permute-start(bf16[16,1024]{1,0:T(8,128)(2,1)S(1)} %collective-permute-done.1), channel_id=1, source_target_pairs={{0,1},{1,2},{2,3},{3,0},{4,5},{5,6},{6,7},{7,4},{8,9},{9,10},{10,1... | collective-permute-start | bytes 98312 | tf_op jit(solution)/shard_map/ppermute | solution.py:26
Sparse Core Ops, SparseCore 0:
  13.2 13.0 reduce-scatter.3
  28.5 10.3 reduce-scatter.5
  51.3 53.4 reduce-scatter.7
